TPU v7x, 256 devices: a whole 4x4x8 slice. The times are simulated.
256 devices in a mesh: seq: 32 (over y, z), tp: 8 (over x, core).
Axes of the slice: x: 4, y: 4, z: 8, core: 2. Of those that a mesh axis runs over, the one named last changes fastest.
Arguments:
- tokens: bfloat16 [24576, 2048], P('seq', 'tp'), may hold values from -20 to 20
- w_query: bfloat16 [2048, 2048], P(None, 'tp'), may hold values from -0.125 to 0.125
- w_key: bfloat16 [2048, 2048], P(None, 'tp'), may hold values from -0.125 to 0.125
- w_value: bfloat16 [2048, 2048], P(None, 'tp'), may hold values from -0.125 to 0.125
- head_gain: float32 [2048], P('tp'), may hold values from 0.5 to 1.5
- w_out: bfloat16 [2048, 2048], P('tp'), may hold values from -0.125 to 0.125
- norm_gain: float32 [2048], replicated, may hold values from 0.5 to 1.5
- w_gate: bfloat16 [2048, 8192], P('seq', 'tp'), may hold values from -0.125 to 0.125
- w_up: bfloat16 [2048, 8192], P('seq', 'tp'), may hold values from -0.125 to 0.125
- w_down: bfloat16 [8192, 2048], P('tp', 'seq'), may hold values from -0.0625 to 0.0625
Outputs:
- layer_out: bfloat16 [24576, 2048], P('seq', 'tp')
All inputs are finite; a program needn't handle non-finite values.
Results may differ from a plain program's by a relative error of at most 0.009.
Values may be sent and summed in bfloat16 or wider, within the bound.
No kernel may reach another device: no remote copies, remote signals or barrier semaphores. Data moves between devices by JAX's collectives and lax.ppermute only.
A program may use at most 128 MiB of HBM per device.

v0:
```python
import jax
import jax.numpy as jnp
from jax import lax
from jax.sharding import Mesh
from jax.sharding import PartitionSpec as P

HD = 128
SEQ = ("seq_0", "seq_1")


def nothing_yet(array, identity):
    return jnp.zeros_like(array) + jnp.asarray(identity, array.dtype)


def entering(array, axes, combine, identity):
    before = start = nothing_yet(array, identity)
    total = array
    for axis in reversed(axes):
        peers, position = (lax.axis_size(axis), lax.axis_index(axis))
        pieces = lax.all_gather(total.astype(jnp.bfloat16), axis)
        inside, total = (start, start)
        for k in range(peers):
            passed = k < position
            total = combine(total, pieces[k].astype(array.dtype))
            inside = jnp.where(passed, total, inside)
        before = combine(inside, before)
    return before


def in_one_piece(arrays, axis, dim, along):
    ends, at = ([], 0)
    for a in arrays[:-1]:
        at += a.shape[along]
        ends.append(at)
    both = jnp.concatenate(arrays, axis=along)
    return tuple(jnp.split(lax.all_gather(both, axis, axis=dim, tiled=True), ends, axis=along))


def split_up(array, dim, peers):
    shape = array.shape
    tiles = array.reshape(*shape[:dim], peers, shape[dim] // peers, *shape[dim + 1 :])
    return jnp.moveaxis(tiles, dim, 0)


def sum_at_owner(array, axis, dim):
    tiles = split_up(array, dim, lax.axis_size(axis))
    arrived = lax.all_to_all(tiles, axis, split_axis=0, concat_axis=0, tiled=True)
    return arrived.astype(jnp.float32).sum(axis=0)


def add_states(earlier, later):
    return earlier + later


def body(tokens, w_query, w_key, w_value, head_gain, w_out, norm_gain, w_gate, w_up, w_down):
    length = tokens.shape[0]
    width_here = tokens.shape[1]
    heads_here = w_query.shape[1] // HD
    features = lax.all_gather(tokens, "tp", axis=1, tiled=True)

    def project(weight):
        product = jnp.dot(features, weight, preferred_element_type=jnp.float32)
        return product.astype(jnp.bfloat16).reshape(length, heads_here, HD)

    query = project(w_query)
    keys_local = project(w_key)
    values_local = project(w_value)
    scores = jnp.einsum("ihd,jhd->hij", query, keys_local, preferred_element_type=jnp.float32)
    causal = jnp.arange(length)[:, None] >= jnp.arange(length)[None, :]
    scores = jnp.where(causal[None], scores, 0.0).astype(jnp.bfloat16)
    inside = jnp.einsum("hij,jhd->ihd", scores, values_local, preferred_element_type=jnp.float32)
    own_state = jnp.einsum(
        "jhd,jhe->hde", keys_local, values_local, preferred_element_type=jnp.float32
    )
    history = entering(own_state, SEQ, add_states, jnp.zeros_like(own_state))
    carried = jnp.einsum(
        "ihd,hde->ihe", query, history.astype(jnp.bfloat16), preferred_element_type=jnp.float32
    )
    mixed = inside + carried
    scale = lax.rsqrt(jnp.mean(mixed * mixed, axis=-1, keepdims=True) + 1e-06)
    normed = (mixed * scale * head_gain.reshape(heads_here, HD)).astype(jnp.bfloat16)
    normed = normed.reshape(length, heads_here * HD)
    partial_value = jnp.dot(normed, w_out, preferred_element_type=jnp.float32)
    own_column = lax.axis_index("tp") * width_here
    summed = lax.psum(partial_value.astype(jnp.bfloat16), "tp").astype(jnp.float32)
    resid_whole = features.astype(jnp.float32) + summed
    factor = lax.rsqrt(jnp.mean(resid_whole * resid_whole, axis=-1, keepdims=True) + 1e-05)
    ffn_in = (resid_whole * factor * norm_gain).astype(jnp.bfloat16)
    resid = lax.dynamic_slice_in_dim(resid_whole, own_column, width_here, 1)
    pieces = in_one_piece((w_gate, w_up), SEQ, 0, 1)
    gate_sum = jnp.dot(ffn_in, pieces[0], preferred_element_type=jnp.float32)
    upward_sum = jnp.dot(ffn_in, pieces[1], preferred_element_type=jnp.float32)
    hidden = (jax.nn.silu(gate_sum) * upward_sum).astype(jnp.bfloat16)
    terms = jnp.dot(
        hidden, lax.all_gather(w_down, SEQ, axis=1, tiled=True), preferred_element_type=jnp.float32
    )
    mlp_share = sum_at_owner(terms.astype(jnp.bfloat16), "tp", 1)
    return (resid + mlp_share).astype(jnp.bfloat16)


def solution(mesh):
    finer = Mesh(mesh.devices.reshape(4, 8, mesh.shape["tp"]), ("seq_0", "seq_1", "tp"))
    return jax.shard_map(
        body,
        mesh=finer,
        in_specs=(
            P(SEQ, "tp"),
            P(None, "tp"),
            P(None, "tp"),
            P(None, "tp"),
            P("tp"),
            P("tp", None),
            P(),
            P(SEQ, "tp"),
            P(SEQ, "tp"),
            P("tp", SEQ),
        ),
        out_specs=P(SEQ, "tp"),
        check_vma=False,
    )
```

profile of v0, /device:TPU:1, one launch (start us, length us, event | category | flops | bytes accessed | tf_op | source)
XLA Modules:
  0.0 356.1 jit_solution(3774338087254047791)
XLA Ops:
  7.4 0.7 all-gather.5.cloned.1.call-update
  8.2 0.2 iota_compare_fusion
  8.3 39.5 %all-gather.5.cloned.1.call-done = bf16[768,2048]{1,0:T(8,128)(2,1)} async-done(((bf16[768,256]{1,0:T(8,128)(2,1)}), bf16[768,2048]{1,0:T(8,128)(2,1)}) %all-gather.5.cloned.1.call-update) | async-done | bytes 3145744 | tf_op jit(solution)/shard_map/all_gather | solution.py:59
  47.9 3.3 convolution_convert_fusion.2
  51.2 2.4 convolution_convert_fusion.4
  53.6 0.3 convolution_convert_fusion.5
  53.9 20.8 %all-gather = bf16[16,128,128]{2,1,0:T(8,128)(2,1)S(1)} all-gather(bf16[2,128,128]{2,1,0:T(8,128)(2,1)S(1)} %convolution_convert_fusion.5), channel_id=2, replica_groups=mesh['seq_0'=4,'seq_1'=8,'tp'=8] {'seq_1'}, dimensions={0}, use_global_device_ids=true | all-gather | bytes 589824 | tf_op jit(solution)/shard_map/all_gather | solution.py:20
  74.7 0.1 fusion.28
  74.7 9.7 %all_gather.22 = bf16[4,2,128,128]{3,2,1,0:T(8,128)(2,1)S(1)} all-gather(bf16[1,2,128,128]{3,2,1,0:T(8,128)(2,1)S(1)} %fusion.28), channel_id=1, replica_groups=mesh['seq_0'=4,'seq_1'=8,'tp'=8] {'seq_0'}, dimensions={0}, use_global_device_ids=true | all-gather | bytes 327680 | tf_op jit(solution)/shard_map/all_gather | solution.py:20
  84.5 1.1 convolution_convert_fusion.3
  85.6 0.7 copy-done.7
  86.3 1.3 fusion.29
  87.6 2.9 multiply_reduce_fusion.1
  90.5 0.1 multiply_convert_fusion.2
  90.6 2.7 convolution_convert_fusion.1
  93.4 0.0 all-gather.7.cloned.1.call-start
  93.5 0.8 copy-done.2
  94.3 0.1 copy-done.3
  94.3 0.7 pad_maximum_fusion
  95.1 0.2 all-gather.9.cloned.1.call-start
  95.3 0.4 all-gather.9.cloned.1.call-update
  95.7 79.1 %all-reduce.2.cloned.1.call-done = bf16[768,2048]{1,0:T(8,128)(2,1)} async-done(((bf16[768,2048]{1,0:T(8,128)(2,1)}), bf16[768,2048]{1,0:T(8,128)(2,1)}) %all-reduce.2.cloned.1.call-update) | async-done | bytes 3145744 | tf_op jit(solution)/shard_map/psum | solution.py:85
  174.8 6.7 %convert_add_fusion = (f32[768,2048]{1,0:T(8,128)}, f32[768]{0:T(1024)S(1)}) fusion(bf16[768,2048]{1,0:T(8,128)(2,1)} %all-reduce.2.cloned.1.call-done, bf16[768,2048]{1,0:T(8,128)(2,1)} %all-gather.5.cloned.1.call-done), kind=kLoop, calls=%fused_computation.3 | loop fusion | flops 7863552 | bytes 12585984 | tf_op jit(solution)/shard_map/add | solution.py:86
  181.6 19.3 %all-gather.7.cloned.1.call-done = bf16[2048,2048]{1,0:T(8,128)(2,1)} async-done(((bf16[64,2048]{1,0:T(8,128)(2,1)}), bf16[2048,2048]{1,0:T(8,128)(2,1)}) %all-gather.7.cloned.1.call-update) | async-done | bytes 8388624 | tf_op jit(solution)/shard_map/all_gather | solution.py:36
  200.9 9.2 %fusion = f32[768,1024]{1,0:T(8,128)} fusion(bf16[2048,2048]{1,0:T(8,128)(2,1)} %all-gather.7.cloned.1.call-done, f32[2048]{0:T(1024)S(1)} %copy-done.6, f32[768]{0:T(1024)S(1)} %add_rsqrt_fusion.1, bf16[768,2048]{1,0:T(8,128)(2,1)} %all-reduce.2.cloned.1.call-done, bf16[768,2048]{1,0:T(8,128)(2,1)} %all-gather.5.cloned.1.call-done), kind=kOutput, calls=%fused_computation.5 | convolution fusion | flops 3230662656 | bytes 13642752 | tf_op jit(solution)/shard_map/dot_general | solution.py:92
  210.2 69.3 %all-gather.9.cloned.1.call-done = bf16[1024,2048]{0,1:T(8,128)(2,1)} async-done(((bf16[1024,64]{0,1:T(8,128)(2,1)}), bf16[1024,2048]{0,1:T(8,128)(2,1)}) %all-gather.9.cloned.1.call-update) | async-done | bytes 4194320 | tf_op jit(solution)/shard_map/all_gather | solution.py:95
  279.5 14.9 %convolution_convert_fusion = bf16[768,2048]{1,0:T(8,128)(2,1)} fusion(bf16[1024,2048]{0,1:T(8,128)(2,1)} %all-gather.9.cloned.1.call-done, f32[768,1024]{1,0:T(8,128)} %fusion, bf16[2048,2048]{1,0:T(8,128)(2,1)} %all-gather.7.cloned.1.call-done, f32[2048]{0:T(1024)S(1)} %copy-done.6, f32[768]{0:T(1024)S(1)} %add_rsqrt_fusion.1, ...), kind=kOutput, calls=%fused_computation.9 | convolution fusion | flops 6458179584 | bytes 20982784 | tf_op jit(solution)/shard_map/dot_general | solution.py:94
  294.4 3.7 %copy.23 = bf16[96,8,8,256]{3,2,0,1:T(8,128)(2,1)} copy(bf16[96,8,8,256]{3,2,1,0:T(8,128)(2,1)} %bitcast.58) | data formatting | bytes 6291456 | tf_op jit(solution)/shard_map/reshape | solution.py:41
  298.1 8.6 %all-to-all-start = ((bf16[8,768,256]{2,1,0:T(8,128)(2,1)}), bf16[8,768,256]{2,1,0:T(8,128)(2,1)}, u32[]{:S(2)}, u32[]{:S(2)}) async-start(bf16[8,768,256]{2,1,0:T(8,128)(2,1)} %bitcast.57), calls=%async_computation | async-start | bytes 6291456 | tf_op jit(solution)/shard_map/all_to_all | solution.py:47
  306.7 37.6 %all-to-all-done = bf16[8,768,256]{2,1,0:T(8,128)(2,1)} async-done(((bf16[8,768,256]{2,1,0:T(8,128)(2,1)}), bf16[8,768,256]{2,1,0:T(8,128)(2,1)}, u32[]{:S(2)}, u32[]{:S(2)}) %all-to-all-start) | async-done | bytes 3145760 | tf_op jit(solution)/shard_map/all_to_all | solution.py:47
  344.3 2.4 convert_reduce_fusion
  346.7 2.0 add_convert_fusion
  (19 shorter events, 0.1 us)
Async XLA Ops:
  7.4 83.3 %copy-start = (bf16[256,2048]{1,0:T(8,128)(2,1)S(1)}, bf16[256,2048]{1,0:T(8,128)(2,1)}, u32[]{:S(2)}) copy-start(bf16[256,2048]{1,0:T(8,128)(2,1)} %param.15) | copy-start | bytes 3145732
  7.4 40.5 %all-gather.5.cloned.1.call-start = ((), (), s32[]{:S(2)}) async-start(), calls=%async_computation.1 | async-start | bytes 3538944 | tf_op jit(solution)/shard_map/all_gather | solution.py:59
  8.1 166.7 %all-reduce.2.cloned.1.call-start = ((), (), s32[]{:S(2)}) async-start(), calls=%async_computation.2 | async-start | bytes 6291456 | tf_op jit(solution)/shard_map/psum | solution.py:85
  47.9 3.4 copy-start.1
  51.2 33.2 %copy-start.5 = (bf16[2048,256]{1,0:T(8,128)(2,1)S(1)}, bf16[2048,256]{1,0:T(8,128)(2,1)}, u32[]{:S(2)}) copy-start(bf16[2048,256]{1,0:T(8,128)(2,1)} %param.11) | copy-start | bytes 3145732
  85.6 0.7 copy-start.7
  87.6 2.9 copy-start.4
  93.4 0.9 copy-start.2
  93.4 1.0 copy-start.3
  93.4 107.5 %all-gather.7.cloned.1.call-start = ((), (), s32[]{:S(2)}) async-start(), calls=%async_computation.3 | async-start | bytes 8650752 | tf_op jit(solution)/shard_map/all_gather | solution.py:36
  95.1 184.4 %all-gather.9.cloned.1.call-start = ((), (), s32[]{:S(2)}) async-start(), calls=%async_computation.4 | async-start | bytes 4325376 | tf_op jit(solution)/shard_map/all_gather | solution.py:95
  95.7 105.2 %copy-start.6 = (f32[2048]{0:T(1024)S(1)}, f32[2048]{0:T(1024)}, u32[]{:S(2)}) copy-start(f32[2048]{0:T(1024)} %param.16) | copy-start | bytes 24580
  298.1 46.2 %all-to-all-start = ((bf16[8,768,256]{2,1,0:T(8,128)(2,1)}), bf16[8,768,256]{2,1,0:T(8,128)(2,1)}, u32[]{:S(2)}, u32[]{:S(2)}) async-start(bf16[8,768,256]{2,1,0:T(8,128)(2,1)} %bitcast.57), calls=%async_computation | async-start | bytes 6291456 | tf_op jit(solution)/shard_map/all_to_all | solution.py:47
Sparse Core Ops, SparseCore 0:
  10.0 37.8 all-gather.4
  93.5 81.2 all-reduce.1
Sparse Core Ops, SparseCore 1:
  96.5 104.4 all-gather.6
  203.4 76.1 all-gather.8
where the time goes:
time: 356 us
  waiting for transfers between devices  246 us (69%)
  matrix products  38.1 us (11%)
  blocking collectives  30.5 us (9%)
  between operations  15 us (4%)
  other arithmetic  12.2 us (3%)
  starting transfers between devices  8.92 us (3%)
  local copies, waits for them, and re-layouts  5.37 us (2%)
    psum x1, waiting for transfers between devices, body(): lax.psum(partial_value.astype(jnp.bfloat16), 'tp').astype(jnp.float32)  79.1 us
    all_gather x1, waiting for transfers between devices, body(): lax.all_gather(w_down, SEQ, axis=1, tiled=True)  69.3 us
    all_gather x1, waiting for transfers between devices, body(): features = lax.all_gather(tokens, 'tp', axis=1, tiled=True)  39.5 us
    all_to_all x1, waiting for transfers between devices, sum_at_owner(): lax.all_to_all(tiles, axis, split_axis=0, concat_axis=0, tiled=True)  37.6 us
    all_gather x2, blocking collectives, entering(): pieces = lax.all_gather(total.astype(jnp.bfloat16), axis)  30.5 us
    all_gather x1, waiting for transfers between devices, in_one_piece(): lax.all_gather(both, axis, axis=dim, tiled=True)  19.3 us
    dot_general x1, matrix products, body(): jnp.dot(hidden, lax.all_gather(w_down, SEQ, axis=1, tiled=True), preferre...  14.9 us
    dot_general x1, matrix products, body(): upward_sum = jnp.dot(ffn_in, pieces[1], preferred_element_type=jnp.float32)  9.24 us
  transfers between devices with their start and end apart: 5, of which 5 were waited for; matrix products, arithmetic and copies ran while one was open for 5% of the time, Pallas kernels for 0%

commit v1 on v0

--- a/solution.py
+++ b/solution.py
@@ -82,7 +82,9 @@
     normed = normed.reshape(length, heads_here * HD)
     partial_value = jnp.dot(normed, w_out, preferred_element_type=jnp.float32)
     own_column = lax.axis_index("tp") * width_here
-    summed = lax.psum(partial_value.astype(jnp.bfloat16), "tp").astype(jnp.float32)
+    summed = jnp.sum(lax.all_gather(partial_value.astype(jnp.bfloat16), "tp"), axis=0).astype(
+        jnp.float32
+    )
     resid_whole = features.astype(jnp.float32) + summed
     factor = lax.rsqrt(jnp.mean(resid_whole * resid_whole, axis=-1, keepdims=True) + 1e-05)
     ffn_in = (resid_whole * factor * norm_gain).astype(jnp.bfloat16)

time: 356 us -> 478 us (1.34)
  waiting for transfers between devices: 246 us -> 354 us
  other arithmetic: 12.2 us -> 27.7 us
    all_gather x0 -> x1, waiting for transfers between devices: none -> 129 us  [body(): lax.all_gather(partial_value.astype(jnp.bfloat16), 'tp')]
    psum x1 -> x0, waiting for transfers between devices: 79.1 us -> none  [body(): lax.psum(partial_value.astype(jnp.bfloat16), 'tp').astype(jnp.float32)]
    all_gather x1, waiting for transfers between devices: 19.3 us -> 78.1 us  [in_one_piece(): lax.all_gather(both, axis, axis=dim, tiled=True)]
    reduce_sum x0 -> x1, other arithmetic: none -> 15.6 us  [body(): jnp.sum(lax.all_gather(partial_value.astype(jnp.bfloat16), 'tp'), axis=0)]
  transfers between devices with their start and end apart: 5 -> 5, of which waited for: 5 -> 5; matrix products, arithmetic and copies ran while one was open for 5% -> 7% of each run, Pallas kernels for 0% -> 0%
where the time goes in v1:
time: 478 us
  waiting for transfers between devices  354 us (74%)
  matrix products  38 us (8%)
  blocking collectives  30.5 us (6%)
  other arithmetic  27.7 us (6%)
  between operations  13.3 us (3%)
  starting transfers between devices  8.85 us (2%)
  local copies, waits for them, and re-layouts  5.41 us (1%)
    all_gather x1, waiting for transfers between devices, body(): lax.all_gather(partial_value.astype(jnp.bfloat16), 'tp')  129 us
    all_gather x1, waiting for transfers between devices, in_one_piece(): lax.all_gather(both, axis, axis=dim, tiled=True)  78.1 us
    all_gather x1, waiting for transfers between devices, body(): lax.all_gather(w_down, SEQ, axis=1, tiled=True)  69.3 us
    all_gather x1, waiting for transfers between devices, body(): features = lax.all_gather(tokens, 'tp', axis=1, tiled=True)  39.5 us
    all_to_all x1, waiting for transfers between devices, sum_at_owner(): lax.all_to_all(tiles, axis, split_axis=0, concat_axis=0, tiled=True)  37.6 us
    all_gather x2, blocking collectives, entering(): pieces = lax.all_gather(total.astype(jnp.bfloat16), axis)  30.5 us
    reduce_sum x1, other arithmetic, body(): jnp.sum(lax.all_gather(partial_value.astype(jnp.bfloat16), 'tp'), axis=0)  15.6 us
    dot_general x1, matrix products, body(): jnp.dot(hidden, lax.all_gather(w_down, SEQ, axis=1, tiled=True), preferre...  14.9 us
  transfers between devices with their start and end apart: 5, of which 5 were waited for; matrix products, arithmetic and copies ran while one was open for 7% of the time, Pallas kernels for 0%

profile of v1, /device:TPU:1, one launch (start us, length us, event | category | flops | bytes accessed | tf_op | source)
XLA Modules:
  0.0 477.8 jit_solution(17050135135874007741)
XLA Ops:
  6.5 0.7 all-gather.7.cloned.1.call-update
  7.3 0.2 iota_compare_fusion
  7.5 39.5 %all-gather.7.cloned.1.call-done = bf16[768,2048]{1,0:T(8,128)(2,1)} async-done(((bf16[768,256]{1,0:T(8,128)(2,1)}), bf16[768,2048]{1,0:T(8,128)(2,1)}) %all-gather.7.cloned.1.call-update) | async-done | bytes 3145744 | tf_op jit(solution)/shard_map/all_gather | solution.py:59
  47.0 3.3 convolution_convert_fusion.4
  50.4 2.4 convolution_convert_fusion.2
  52.8 0.3 convolution_convert_fusion.5
  53.1 20.8 %all-gather = bf16[16,128,128]{2,1,0:T(8,128)(2,1)S(1)} all-gather(bf16[2,128,128]{2,1,0:T(8,128)(2,1)S(1)} %convolution_convert_fusion.5), channel_id=2, replica_groups=mesh['seq_0'=4,'seq_1'=8,'tp'=8] {'seq_1'}, dimensions={0}, use_global_device_ids=true | all-gather | bytes 589824 | tf_op jit(solution)/shard_map/all_gather | solution.py:20
  73.8 0.1 fusion.28
  73.9 9.7 %all_gather.28 = bf16[4,2,128,128]{3,2,1,0:T(8,128)(2,1)S(1)} all-gather(bf16[1,2,128,128]{3,2,1,0:T(8,128)(2,1)S(1)} %fusion.28), channel_id=1, replica_groups=mesh['seq_0'=4,'seq_1'=8,'tp'=8] {'seq_0'}, dimensions={0}, use_global_device_ids=true | all-gather | bytes 327680 | tf_op jit(solution)/shard_map/all_gather | solution.py:20
  83.6 1.1 convolution_convert_fusion.3
  84.7 0.7 copy-done.8
  85.5 1.3 fusion.29
  86.8 2.9 multiply_reduce_fusion.1
  89.7 0.1 multiply_convert_fusion.2
  89.8 2.7 convolution_convert_fusion.1
  92.6 0.8 copy-done.3
  93.4 0.1 copy-done.4
  93.5 0.7 pad_maximum_fusion
  94.3 0.2 all-gather.11.cloned.1.call-start
  94.5 0.3 all-gather.11.cloned.1.call-update
  94.8 128.5 %all-gather.13.cloned.1.call-done = bf16[6144,2048]{1,0:T(8,128)(2,1)} async-done(((bf16[768,2048]{1,0:T(8,128)(2,1)}), bf16[6144,2048]{1,0:T(8,128)(2,1)}) %all-gather.13.cloned.1.call-update) | async-done | bytes 25165840 | tf_op jit(solution)/shard_map/all_gather | solution.py:85
  223.3 15.6 %reduce_sum.40 = bf16[768,2048]{1,0:T(8,128)(2,1)} reduce(bf16[8,768,2048]{2,1,0:T(8,128)(2,1)} %bitcast.58, bf16[]{:T(256)} %constant.44.clone.1), dimensions={0}, to_apply=%region_1.2 | reduce | flops 11010048 | bytes 28311554 | tf_op jit(solution)/shard_map/reduce_sum | solution.py:85
  239.0 6.6 %convert_add_fusion = (f32[768,2048]{1,0:T(8,128)}, f32[768]{0:T(1024)S(1)}) fusion(bf16[768,2048]{1,0:T(8,128)(2,1)} %reduce_sum.40, bf16[768,2048]{1,0:T(8,128)(2,1)} %all-gather.7.cloned.1.call-done), kind=kLoop, calls=%fused_computation.3 | loop fusion | flops 7863552 | bytes 12585984 | tf_op jit(solution)/shard_map/add | solution.py:88
  245.6 78.1 %all-gather.9.cloned.1.call-done = bf16[2048,2048]{1,0:T(8,128)(2,1)} async-done(((bf16[64,2048]{1,0:T(8,128)(2,1)}), bf16[2048,2048]{1,0:T(8,128)(2,1)}) %all-gather.9.cloned.1.call-update) | async-done | bytes 8388624 | tf_op jit(solution)/shard_map/all_gather | solution.py:36
  323.7 9.2 %fusion = f32[768,1024]{1,0:T(8,128)} fusion(bf16[2048,2048]{1,0:T(8,128)(2,1)} %all-gather.9.cloned.1.call-done, f32[2048]{0:T(1024)S(1)} %copy-done.7, f32[768]{0:T(1024)S(1)} %add_rsqrt_fusion.1, bf16[768,2048]{1,0:T(8,128)(2,1)} %reduce_sum.40, bf16[768,2048]{1,0:T(8,128)(2,1)} %all-gather.7.cloned.1.call-done), kind=kOutput, calls=%fused_computation.5 | convolution fusion | flops 3230662656 | bytes 13642752 | tf_op jit(solution)/shard_map/dot_general | solution.py:94
  332.9 69.3 %all-gather.11.cloned.1.call-done = bf16[1024,2048]{0,1:T(8,128)(2,1)} async-done(((bf16[1024,64]{0,1:T(8,128)(2,1)}), bf16[1024,2048]{0,1:T(8,128)(2,1)}) %all-gather.11.cloned.1.call-update) | async-done | bytes 4194320 | tf_op jit(solution)/shard_map/all_gather | solution.py:97
  402.2 14.9 %convolution_convert_fusion = bf16[768,2048]{1,0:T(8,128)(2,1)} fusion(bf16[1024,2048]{0,1:T(8,128)(2,1)} %all-gather.11.cloned.1.call-done, f32[768,1024]{1,0:T(8,128)} %fusion, bf16[2048,2048]{1,0:T(8,128)(2,1)} %all-gather.9.cloned.1.call-done, f32[2048]{0:T(1024)S(1)} %copy-done.7, f32[768]{0:T(1024)S(1)} %add_rsqrt_fusion.1, ...), kind=kOutput, calls=%fused_computation.9 | convolution fusion | flops 6458179584 | bytes 20982784 | tf_op jit(solution)/shard_map/dot_general | solution.py:96
  417.0 3.7 copy.23
  420.8 8.5 %all-to-all-start = ((bf16[8,768,256]{2,1,0:T(8,128)(2,1)}), bf16[8,768,256]{2,1,0:T(8,128)(2,1)}, u32[]{:S(2)}, u32[]{:S(2)}) async-start(bf16[8,768,256]{2,1,0:T(8,128)(2,1)} %bitcast.59), calls=%async_computation | async-start | bytes 6291456 | tf_op jit(solution)/shard_map/all_to_all | solution.py:47
  429.3 37.6 %all-to-all-done = bf16[8,768,256]{2,1,0:T(8,128)(2,1)} async-done(((bf16[8,768,256]{2,1,0:T(8,128)(2,1)}), bf16[8,768,256]{2,1,0:T(8,128)(2,1)}, u32[]{:S(2)}, u32[]{:S(2)}) %all-to-all-start) | async-done | bytes 3145760 | tf_op jit(solution)/shard_map/all_to_all | solution.py:47
  466.9 2.4 convert_reduce_fusion
  469.3 2.0 add_convert_fusion
  (22 shorter events, 0.2 us)
Async XLA Ops:
  6.5 83.3 %copy-start = (bf16[256,2048]{1,0:T(8,128)(2,1)S(1)}, bf16[256,2048]{1,0:T(8,128)(2,1)}, u32[]{:S(2)}) copy-start(bf16[256,2048]{1,0:T(8,128)(2,1)} %param.15) | copy-start | bytes 3145732
  6.5 40.5 %all-gather.7.cloned.1.call-start = ((), (), s32[]{:S(2)}) async-start(), calls=%async_computation.1 | async-start | bytes 3538944 | tf_op jit(solution)/shard_map/all_gather | solution.py:59
  7.3 216.1 %all-gather.13.cloned.1.call-start = ((), (), s32[]{:S(2)}) async-start(), calls=%async_computation.4 | async-start | bytes 28311552 | tf_op jit(solution)/shard_map/all_gather | solution.py:85
  47.0 3.3 copy-start.2
  50.4 33.3 %copy-start.6 = (bf16[2048,256]{1,0:T(8,128)(2,1)S(1)}, bf16[2048,256]{1,0:T(8,128)(2,1)}, u32[]{:S(2)}) copy-start(bf16[2048,256]{1,0:T(8,128)(2,1)} %param.11) | copy-start | bytes 3145732
  84.7 0.7 copy-start.8
  86.8 2.9 copy-start.5
  92.5 0.9 copy-start.3
  92.5 1.0 copy-start.4
  92.6 231.1 %all-gather.9.cloned.1.call-start = ((), (), s32[]{:S(2)}) async-start(), calls=%async_computation.2 | async-start | bytes 8650752 | tf_op jit(solution)/shard_map/all_gather | solution.py:36
  94.3 307.9 %all-gather.11.cloned.1.call-start = ((), (), s32[]{:S(2)}) async-start(), calls=%async_computation.3 | async-start | bytes 4325376 | tf_op jit(solution)/shard_map/all_gather | solution.py:97
  239.0 84.7 %copy-start.7 = (f32[2048]{0:T(1024)S(1)}, f32[2048]{0:T(1024)}, u32[]{:S(2)}) copy-start(f32[2048]{0:T(1024)} %param.16) | copy-start | bytes 24580
  420.8 46.1 %all-to-all-start = ((bf16[8,768,256]{2,1,0:T(8,128)(2,1)}), bf16[8,768,256]{2,1,0:T(8,128)(2,1)}, u32[]{:S(2)}, u32[]{:S(2)}) async-start(bf16[8,768,256]{2,1,0:T(8,128)(2,1)} %bitcast.59), calls=%async_computation | async-start | bytes 6291456 | tf_op jit(solution)/shard_map/all_to_all | solution.py:47
  429.3 42.0 %copy-start.1 = (bf16[256,2048]{1,0:T(8,128)(2,1)S(1)}, bf16[256,2048]{1,0:T(8,128)(2,1)}, u32[]{:S(2)}) copy-start(bf16[256,2048]{1,0:T(8,128)(2,1)} %param.15) | copy-start | bytes 3145732
Sparse Core Ops, SparseCore 0:
  9.2 37.8 all-gather.6
  92.7 130.6 all-gather.12
  225.9 97.6 all-gather.8
  326.1 76.0 all-gather.10
